TPU v7x, 8 devices: a whole 2x2x1 slice. The times are simulated.
8 devices in a mesh: dp: 1 (over z), cp: 8 (over y, x, core).
Axes of the slice: x: 2, y: 2, z: 1, core: 2. Of those that a mesh axis runs over, the one named last changes fastest.
Arguments:
- x_in: bfloat16 [8192, 3584], P(('dp', 'cp'))
- dy_in: bfloat16 [8192, 3584], P(('dp', 'cp'))
- doc_id: int32 [8192], P(('dp', 'cp'))
- w_q: bfloat16 [3584, 2, 256], replicated
- w_k: bfloat16 [3584, 1, 256], replicated
- w_v: bfloat16 [3584, 1, 256], replicated
- w_o: bfloat16 [2, 256, 3584], replicated
Outputs:
- output 1: bfloat16 [8192, 3584], P(('dp', 'cp'))
- output 2: bfloat16 [8192, 3584], P(('dp', 'cp'))
All inputs are finite; a program needn't handle non-finite values.
Results may differ from a plain program's by a relative error of at most 0.00929256.
Values are sent between devices in bfloat16 or wider.
A program may use at most 1 GiB of HBM per device.

v0:
```python
import functools
import math

import jax
import jax.numpy as jnp
from jax import lax
from jax.experimental import pallas as pl
from jax.experimental.pallas import tpu as pltpu
from jax.sharding import PartitionSpec as P


NEG_BIG = -1.0e30
BF16 = jnp.bfloat16
F32 = jnp.float32
PIECE = 512
ROWS = 256
LANES = 128
NT = (((1,), (1,)), ((), ()))
NN = (((1,), (0,)), ((), ()))
VMEM_LIMIT = 60 * 1024 * 1024
MESH = pl.DeviceIdType.MESH
ANY = pl.BlockSpec(memory_space=pl.ANY)
VMEM = pl.BlockSpec(memory_space=pltpu.VMEM)


def dot(a, b, dims):
    return lax.dot_general(a, b, dims, preferred_element_type=F32)


def doc_start(bounds, pos):
    out = jnp.zeros_like(pos)
    for b in bounds:
        out = jnp.maximum(out, jnp.where(b <= pos, b, 0))
    return out


def doc_end(bounds, pos, seq_len):
    out = seq_len
    for b in bounds:
        out = jnp.minimum(out, jnp.where(b > pos, b, seq_len))
    return out


def neighbours(me):
    return me + 2 - 4 * ((me // 2) % 2), me + 4 - 8 * (me // 4), me + 1 - 2 * (me % 2)


def entry_barrier(me, n_dev):
    barrier = pltpu.get_barrier_semaphore()
    for d in range(1, n_dev):
        pl.semaphore_signal(barrier, inc=1, device_id={'cp': lax.rem(me + d, n_dev)}, device_id_type=MESH)
    pl.semaphore_wait(barrier, n_dev - 1)


def broadcast_copies(me, n_dev, src, dst, send_sem, recv_sem):
    return [
        pltpu.make_async_remote_copy(
            src_ref=src, dst_ref=dst.at[me], send_sem=send_sem.at[d - 1], recv_sem=recv_sem.at[d - 1],
            device_id={'cp': lax.rem(me + d, n_dev)}, device_id_type=MESH)
        for d in range(1, n_dev)
    ]


def proj_gather_kernel(n_dev, x_hbm, dy_hbm, doc_ref, wq_hbm, wk_hbm, wv_hbm, wo_hbm,
                       kvg, own_hbm, par_hbm, up_hbm, w_hbm, sc_ref,
                       x_s, dy_s, wq_s, w_s, wo_s, kv_s, qd_s, docg_ref,
                       w_sem, x_sem, dy_sem, send_sem, recv_sem, qsend_sem, qrecv_sem, loc_sem, dsend_sem, drecv_sem):
    me = lax.axis_index('cp')
    px, py, pc = neighbours(me)
    pd = px + py - me
    last = 2 * n_dev - 1
    hd = wq_s.shape[2]
    qd = 2 * hd
    tiles = PIECE // ROWS

    w_copies = [pltpu.make_async_copy(a, b, w_sem.at[n]) for n, (a, b) in enumerate(
        ((wk_hbm, w_s.at[:, pl.ds(qd, hd)]), (wv_hbm, w_s.at[:, pl.ds(qd + hd, hd)]), (wq_hbm, wq_s), (wo_hbm, wo_s)))]

    def row_copy(src, dst, sem, tile):
        rows = pl.ds(pl.multiple_of(tile * ROWS, ROWS), ROWS)
        return pltpu.make_async_copy(src.at[rows], dst.at[rows], sem.at[tile])

    w_copies[0].start()
    w_copies[1].start()
    for t in range(2 * tiles):
        row_copy(x_hbm, x_s, x_sem, t).start()
    w_copies[2].start()
    w_copies[3].start()
    for t in range(2 * tiles):
        row_copy(dy_hbm, dy_s, dy_sem, t).start()

    entry_barrier(me, n_dev)
    docg_ref[me] = doc_ref[...]
    doc_copies = broadcast_copies(me, n_dev, doc_ref, docg_ref, dsend_sem, drecv_sem)
    for cp in doc_copies:
        cp.start()

    hops = (
        (kv_s.at[0], me, px), (kv_s.at[1], last - me, px),
        (kv_s.at[0], me, py), (kv_s.at[1], last - me, py),
        (kv_s.at[0], me, pc), (kv_s.at[1], last - me, pc),
        (kvg.at[px], px, py), (kvg.at[last - py], last - py, px),
        (kvg.at[px], px, pc), (kvg.at[last - px], last - px, pc),
        (kvg.at[py], py, pc), (kvg.at[last - py], last - py, pc),
        (kvg.at[pd], pd, pc), (kvg.at[last - pd], last - pd, pc),
    )
    copies = [
        pltpu.make_async_remote_copy(
            src_ref=src, dst_ref=kvg.at[piece], send_sem=send_sem.at[n], recv_sem=recv_sem.at[n],
            device_id={'cp': peer}, device_id_type=MESH)
        for n, (src, piece, peer) in enumerate(hops)
    ]
    local = [pltpu.make_async_copy(src, dst, loc_sem.at[n]) for n, (src, dst) in enumerate((
        (kv_s.at[0], kvg.at[me]), (kv_s.at[1], kvg.at[last - me]), (qd_s.at[0], own_hbm.at[0]), (qd_s.at[1], own_hbm.at[1]), (qd_s.at[1], up_hbm), (w_s, w_hbm)))]
    q_copies = [
        pltpu.make_async_remote_copy(
            src_ref=qd_s.at[n], dst_ref=par_hbm.at[n], send_sem=qsend_sem.at[n], recv_sem=qrecv_sem.at[n],
            device_id={'cp': pc}, device_id_type=MESH)
        for n in range(2)
    ]

    def kv_piece(p):
        @pl.loop(0, tiles)
        def _(h):
            row_copy(x_hbm, x_s, x_sem, p * tiles + h).wait()
            rows = pl.ds(pl.multiple_of(p * PIECE + h * ROWS, ROWS), ROWS)
            out = pl.ds(pl.multiple_of(h * ROWS, ROWS), ROWS)
            kv_s[p, out, :] = dot(x_s[rows, :], w_s[:, qd:], NN).astype(BF16)

    def qd_piece(p):
        @pl.loop(0, tiles)
        def _(h):
            rows = pl.ds(pl.multiple_of(p * PIECE + h * ROWS, ROWS), ROWS)
            out = pl.ds(pl.multiple_of(h * ROWS, ROWS), ROWS)
            qd_s[p, out, 0:qd] = dot(x_s[rows, :], w_s[:, :qd], NN).astype(BF16)
            row_copy(dy_hbm, dy_s, dy_sem, p * tiles + h).wait()
            qd_s[p, out, qd:] = dot(dy_s[rows, :], wo_s[...], NT).astype(BF16)

    w_copies[0].wait()
    w_copies[1].wait()
    kv_piece(0)
    copies[0].start()
    copies[4].start()
    local[0].start()
    kv_piece(1)
    for n in (3, 1, 2, 5):
        copies[n].start()
    local[1].start()
    w_copies[2].wait()

    @pl.loop(0, wq_s.shape[0] // PIECE)
    def _(n):
        rows = pl.ds(pl.multiple_of(n * PIECE, PIECE), PIECE)
        w_s[rows, 0:hd] = wq_s[rows, 0, :]
        w_s[rows, hd:qd] = wq_s[rows, 1, :]

    w_copies[3].wait()
    qd_piece(0)
    q_copies[0].start()
    local[2].start()
    qd_piece(1)
    q_copies[1].start()
    for n in (3, 4, 5):
        local[n].start()
    for arrived, forwards in ((0, (6, 8)), (3, (7, 11)), (1, (9,)), (2, (10,)), (6, (12,)), (7, (13,))):
        copies[arrived].wait_recv()
        for n in forwards:
            copies[n].start()
    for n in (4, 5, 8, 9, 10, 11, 12, 13):
        copies[n].wait_recv()
    for cp in copies:
        cp.wait_send()
    for cp in local + q_copies + doc_copies:
        cp.wait()
    docs = docg_ref[...]
    sc_ref[0] = me
    for d in range(1, 5):
        sc_ref[d] = jnp.sum((docs < d).astype(jnp.int32))


def proj_gather(x, dy, doc, wq, wk, wv, wo, n_dev):
    rows, d = x.shape
    hd = wk.shape[1]
    qd_shape = jax.ShapeDtypeStruct((2, PIECE, 4 * hd), BF16)
    dma = pltpu.SemaphoreType.DMA
    n_tile = rows // ROWS
    return pl.pallas_call(
        functools.partial(proj_gather_kernel, n_dev),
        in_specs=[ANY, ANY, VMEM, ANY, ANY, ANY, ANY],
        out_specs=[ANY] * 5 + [pl.BlockSpec(memory_space=pltpu.SMEM)],
        out_shape=[
            jax.ShapeDtypeStruct((2 * n_dev, PIECE, 2 * hd), BF16),
            qd_shape, qd_shape, jax.ShapeDtypeStruct((PIECE, 4 * hd), BF16),
            jax.ShapeDtypeStruct((d, 4 * hd), BF16),
            jax.ShapeDtypeStruct((5,), jnp.int32),
        ],
        scratch_shapes=[
            pltpu.VMEM((rows, d), BF16), pltpu.VMEM((rows, d), BF16),
            pltpu.VMEM(wq.shape, BF16), pltpu.VMEM((d, 4 * hd), BF16), pltpu.VMEM((2 * hd, d), BF16),
            pltpu.VMEM((2, PIECE, 2 * hd), BF16), pltpu.VMEM((2, PIECE, 4 * hd), BF16), pltpu.VMEM((n_dev,) + doc.shape, jnp.int32),
            *(dma((n,)) for n in (4, n_tile, n_tile, 14, 14, 2, 2, 6, n_dev - 1, n_dev - 1)),
        ],
        compiler_params=pltpu.CompilerParams(vmem_limit_bytes=VMEM_LIMIT, collective_id=0, has_side_effects=True),
        cost_estimate=pl.CostEstimate(flops=12 * rows * d * hd, bytes_accessed=8 * rows * d, transcendentals=0),
        name="proj_gather",
    )(x, dy, doc, wq, wk, wv, wo)


def ld_gather_kernel(n_dev, ld_ref, out_ref, send_sem, recv_sem):
    me = lax.axis_index('cp')
    entry_barrier(me, n_dev)
    out_ref[me] = ld_ref[...]
    copies = broadcast_copies(me, n_dev, ld_ref, out_ref, send_sem, recv_sem)
    for cp in copies:
        cp.start()
    for cp in copies:
        cp.wait()


def ld_gather(ld, n_dev):
    return pl.pallas_call(
        functools.partial(ld_gather_kernel, n_dev),
        in_specs=[VMEM], out_specs=VMEM,
        out_shape=jax.ShapeDtypeStruct((n_dev,) + ld.shape, F32),
        scratch_shapes=[pltpu.SemaphoreType.DMA((n_dev - 1,)), pltpu.SemaphoreType.DMA((n_dev - 1,))],
        compiler_params=pltpu.CompilerParams(collective_id=1, has_side_effects=True),
        cost_estimate=pl.CostEstimate(flops=10_000_000, bytes_accessed=1 << 20, transcendentals=0),
        name="ld_gather",
    )(ld)


class Loader:
    def __init__(self, dst, sem, flag):
        self.dst, self.sem, self.flag = dst, sem, flag

    def copy(self, src, piece):
        return pltpu.make_async_copy(src, self.dst.at[piece], self.sem.at[piece])

    def start(self, src, piece, want):
        self.flag[piece] = jnp.where(want, 1, 0)

        @pl.when(self.flag[piece] == 1)
        def _():
            self.copy(src, piece).start()

    def need(self, src, piece):
        @pl.when(self.flag[piece] == 1)
        def _():
            self.copy(src, piece).wait()
            self.flag[piece] = 0


def loader_scratch(n_piece, width):
    return [pltpu.VMEM((n_piece, PIECE, width), BF16), pltpu.SemaphoreType.DMA((n_piece,)), pltpu.SMEM((n_piece,), jnp.int32)]


def key_range(bounds, piece):
    return doc_start(bounds, piece * PIECE) // PIECE, piece + 1


def start_kv(sc_ref, n_dev, bounds, kv_hbm, kv):
    me = sc_ref[0]
    late = 2 * n_dev - 1 - me
    lo_e, lo_l = key_range(bounds, me)[0], key_range(bounds, late)[0]
    for p in range(2 * n_dev):
        kv.start(kv_hbm.at[p], p, ((p >= lo_e) & (p <= me)) | ((p >= lo_l) & (p <= late)))


def fold_lanes(op, acc, s):
    for j in range(s.shape[1] // LANES):
        acc = op(acc, s[:, j * LANES:(j + 1) * LANES])
    return acc


def stack_heads(a, lo, hd):
    return jnp.concatenate([a[:, lo:lo + hd], a[:, lo + hd:lo + 2 * hd]], axis=0)


def fill_starts(bounds, piece, ref):
    ref[...] = doc_start(bounds, piece * PIECE + lax.broadcasted_iota(jnp.int32, ref.shape, 0) % PIECE)


def mask_rows(s, starts, q_first, k_first):
    rpos = q_first + lax.broadcasted_iota(jnp.int32, starts.shape, 0) % PIECE
    lane = k_first + lax.broadcasted_iota(jnp.int32, (1, LANES), 1)
    parts = []
    for j in range(s.shape[1] // LANES):
        kpos = lane + j * LANES
        parts.append(jnp.where((kpos <= rpos) & (kpos >= starts), s[:, j * LANES:(j + 1) * LANES], NEG_BIG))
    return jnp.concatenate(parts, axis=1)


def masked_or_not(bounds, q_piece, k_piece, body):
    whole = (k_piece < q_piece) & (doc_start(bounds, q_piece * PIECE + PIECE - 1) <= k_piece * PIECE)

    @pl.when(whole)
    def _():
        body(False)

    @pl.when(jnp.logical_not(whole))
    def _():
        body(True)


def attn_fwd_kernel(n_dev, scale, sc_ref, q_ref, kv_hbm, o_ref, ld_ref, lcol_ref, dcol_ref,
                    kv_s, kv_sem, kv_flag, s_ref, mx_ref, l_ref, acc_ref, st_ref):
    t = pl.program_id(0)
    bounds = [sc_ref[1 + d] for d in range(4)]
    hd = acc_ref.shape[1]
    c2 = scale * math.log2(math.e)
    kv = Loader(kv_s, kv_sem, kv_flag)

    @pl.when(t == 0)
    def _():
        start_kv(sc_ref, n_dev, bounds, kv_hbm, kv)

    piece = jnp.where(t == 0, sc_ref[0], 2 * n_dev - 1 - sc_ref[0])
    kt0, kt1 = key_range(bounds, piece)
    fill_starts(bounds, piece, st_ref)
    mx_ref[...] = jnp.full(mx_ref.shape, NEG_BIG, F32)

    @pl.loop(kt0, kt1)
    def _(kt):
        kv.need(kv_hbm.at[kt], kt)

        def tile(masked):
            s = dot(stack_heads(q_ref[0], 0, hd), kv_s[kt, :, :hd], NT) * c2
            if masked:
                s = mask_rows(s, st_ref[...], piece * PIECE, kt * PIECE)
            s_ref[kt] = s
            mx_ref[...] = fold_lanes(jnp.maximum, mx_ref[...], s)

        masked_or_not(bounds, piece, kt, tile)

    m = jnp.max(mx_ref[...], axis=1, keepdims=True)
    l_ref[...] = jnp.zeros(l_ref.shape, F32)
    acc_ref[...] = jnp.zeros(acc_ref.shape, F32)

    @pl.loop(kt0, kt1)
    def _(kt):
        p = jnp.exp2(s_ref[kt] - m)
        l_ref[...] = fold_lanes(jnp.add, l_ref[...], p)
        acc_ref[...] += dot(p.astype(BF16), kv_s[kt, :, hd:], NN)

    l = jnp.sum(l_ref[...], axis=1, keepdims=True)
    o2 = (acc_ref[...] * (1.0 / l)).astype(BF16)
    o_ref[:, :hd] = o2[:PIECE]
    o_ref[:, hd:] = o2[PIECE:]
    do2 = stack_heads(q_ref[0], 2 * hd, hd)
    delta = jnp.sum(do2.astype(F32) * o2.astype(F32), axis=1, keepdims=True)
    l2 = jnp.broadcast_to(m + jnp.log2(l), (2 * PIECE, LANES))
    delta = jnp.broadcast_to(delta, (2 * PIECE, LANES))
    lcol_ref[0] = l2
    dcol_ref[0] = delta
    ld_ref[0, 0:1] = jnp.transpose(l2)[0:1]
    ld_ref[0, 1:2] = jnp.transpose(delta)[0:1]


def attn_fwd(sc, q, kvg, n_dev, scale):
    n_piece, _, two_hd = kvg.shape
    hd = two_hd // 2
    col = pl.BlockSpec((1, 2 * PIECE, LANES), lambda t, sc: (t, 0, 0))
    col_shape = jax.ShapeDtypeStruct((2, 2 * PIECE, LANES), F32)
    return pl.pallas_call(
        functools.partial(attn_fwd_kernel, n_dev, scale),
        grid_spec=pltpu.PrefetchScalarGridSpec(
            num_scalar_prefetch=1,
            grid=(2,),
            in_specs=[pl.BlockSpec((1, PIECE, 4 * hd), lambda t, sc: (t, 0, 0)), ANY],
            out_specs=[
                pl.BlockSpec((PIECE, two_hd), lambda t, sc: (t, 0)),
                pl.BlockSpec((1, 2, 2 * PIECE), lambda t, sc: (t, 0, 0)),
                col, col,
            ],
            scratch_shapes=[
                *loader_scratch(n_piece, two_hd),
                pltpu.VMEM((n_piece, 2 * PIECE, PIECE), F32),
                pltpu.VMEM((2 * PIECE, LANES), F32),
                pltpu.VMEM((2 * PIECE, LANES), F32),
                pltpu.VMEM((2 * PIECE, hd), F32),
                pltpu.VMEM((2 * PIECE, LANES), jnp.int32),
            ],
        ),
        out_shape=[
            jax.ShapeDtypeStruct((2 * PIECE, two_hd), BF16),
            jax.ShapeDtypeStruct((2, 2, 2 * PIECE), F32),
            col_shape, col_shape,
        ],
        compiler_params=pltpu.CompilerParams(vmem_limit_bytes=VMEM_LIMIT, dimension_semantics=("arbitrary",)),
        cost_estimate=pl.CostEstimate(flops=8 * n_piece * PIECE * PIECE * hd, bytes_accessed=kvg.size, transcendentals=0),
        name="attn_fwd",
    )(sc, q, kvg)


def attn_dq_kernel(n_dev, scale, sc_ref, q_ref, lcol_ref, dcol_ref, kv_hbm, dq_ref, kv_s, kv_sem, kv_flag, acc_ref, st_ref):
    t = pl.program_id(0)
    bounds = [sc_ref[1 + d] for d in range(4)]
    hd = acc_ref.shape[1]
    c2 = scale * math.log2(math.e)
    kv = Loader(kv_s, kv_sem, kv_flag)

    @pl.when(t == 0)
    def _():
        start_kv(sc_ref, n_dev, bounds, kv_hbm, kv)

    piece = jnp.where(t == 0, sc_ref[0], 2 * n_dev - 1 - sc_ref[0])
    kt0, kt1 = key_range(bounds, piece)
    fill_starts(bounds, piece, st_ref)
    acc_ref[...] = jnp.zeros(acc_ref.shape, F32)

    @pl.loop(kt0, kt1)
    def _(kt):
        kv.need(kv_hbm.at[kt], kt)

        def tile(masked):
            k = kv_s[kt, :, :hd]
            s = dot(stack_heads(q_ref[0], 0, hd), k, NT) * c2 - lcol_ref[0, :, 0:1]
            if masked:
                s = mask_rows(s, st_ref[...], piece * PIECE, kt * PIECE)
            p = jnp.exp2(s).astype(BF16).astype(F32)
            dp = dot(stack_heads(q_ref[0], 2 * hd, hd), kv_s[kt, :, hd:], NT)
            ds = (p * (dp - dcol_ref[0, :, 0:1])).astype(BF16)
            acc_ref[...] += dot(ds, k, NN)

        masked_or_not(bounds, piece, kt, tile)

    dq2 = (acc_ref[...] * scale).astype(BF16)
    dq_ref[:, :hd] = dq2[:PIECE]
    dq_ref[:, hd:] = dq2[PIECE:]


def attn_dq(sc, q, lcol, dcol, kvg, n_dev, scale):
    n_piece, _, two_hd = kvg.shape
    hd = two_hd // 2
    col = pl.BlockSpec((1, 2 * PIECE, LANES), lambda t, sc: (t, 0, 0))
    return pl.pallas_call(
        functools.partial(attn_dq_kernel, n_dev, scale),
        grid_spec=pltpu.PrefetchScalarGridSpec(
            num_scalar_prefetch=1,
            grid=(2,),
            in_specs=[pl.BlockSpec((1, PIECE, 4 * hd), lambda t, sc: (t, 0, 0)), col, col, ANY],
            out_specs=pl.BlockSpec((PIECE, two_hd), lambda t, sc: (t, 0)),
            scratch_shapes=[*loader_scratch(n_piece, two_hd), pltpu.VMEM((2 * PIECE, hd), F32), pltpu.VMEM((2 * PIECE, LANES), jnp.int32)],
        ),
        out_shape=jax.ShapeDtypeStruct((2 * PIECE, two_hd), BF16),
        compiler_params=pltpu.CompilerParams(vmem_limit_bytes=VMEM_LIMIT, dimension_semantics=("arbitrary",)),
        cost_estimate=pl.CostEstimate(flops=12 * n_piece * PIECE * PIECE * hd, bytes_accessed=kvg.size, transcendentals=0),
        name="attn_dq",
    )(sc, q, lcol, dcol, kvg)


def chips_of(me):
    px, py, _ = neighbours(me)
    chip, core = me // 2, me % 2
    return chip, px // 2, py // 2, px // 2 + py // 2 - chip, core


def attn_kv_kernel(n_dev, scale, target, sc_ref, ld_ref, kv_ref, *refs):
    own = target is None
    n_in = 8 if own else 2
    qd_in, (out_ref, qd_s, qd_sem, qd_flag, dk_ref, dv_ref) = refs[:n_in], refs[n_in:]
    g = pl.program_id(0)
    me = sc_ref[0]
    bounds = [sc_ref[1 + d] for d in range(4)]
    hd = dk_ref.shape[1]
    seq_len = 2 * n_dev * PIECE
    last = 2 * n_dev - 1
    c2 = scale * math.log2(math.e)
    chip, x_chip, y_chip, d_chip, core = chips_of(me)
    par = me + 1 - 2 * core
    qd = Loader(qd_s, qd_sem, qd_flag)

    sources = [(qd_in[0].at[0], me, True), (qd_in[0].at[1], last - me, True), (qd_in[1].at[0], par, True), (qd_in[1].at[1], last - par, True)]
    for same, other, c in zip(qd_in[2::2], qd_in[3::2], (x_chip, y_chip, d_chip)):
        sources.append((same, last - (2 * c + core), c < chip))
        sources.append((other, last - (2 * c + 1 - core), c < chip))

    def end_of(piece):
        return (doc_end(bounds, piece * PIECE + PIECE - 1, seq_len) + PIECE - 1) // PIECE

    if own:
        kp = jnp.where(g == 0, me, last - me)
        a0 = jnp.where(g == 0, me, 2 * chip + 2)
        b0 = jnp.where(g == 0, last - 1 - 2 * chip, last - me)
        b1 = last + 1
        live = True
    else:
        tgt = (x_chip, y_chip, d_chip)[target]
        kp = 2 * tgt + core
        a0 = 2 * chip
        b0 = last - 1 - 2 * chip
        b1 = b0 + 2
        live = tgt < chip
    end = end_of(kp)

    @pl.when(g == 0)
    def _():
        for ref, piece, valid in sources:
            if not own:
                valid = live & (piece < end)
            else:
                valid = valid & (((piece >= me) & (piece < end_of(me))) | ((piece >= last - me) & (piece < end_of(last - me))))
            qd.start(ref, piece, valid)

    na = jnp.maximum(jnp.minimum(2 * chip + 2, end) - a0, 0)
    nb = jnp.maximum(jnp.minimum(b1, end) - b0, 0)
    dk_ref[...] = jnp.zeros(dk_ref.shape, F32)
    dv_ref[...] = jnp.zeros(dv_ref.shape, F32)

    @pl.loop(0, jnp.where(live, na + nb, 0))
    def _(i):
        qp = jnp.where(i < na, a0 + i, b0 + i - na)
        qd.need(sources[0][0], qp)
        slot = jnp.where(qp < n_dev, 2 * qp, 2 * (last - qp) + 1)

        def tile(masked):
            q = qd_s[qp]
            q2, do2 = stack_heads(q, 0, hd), stack_heads(q, 2 * hd, hd)
            s = dot(kv_ref[0, :, :hd], q2, NT) * c2 - ld_ref[slot, 0:1, :]
            if masked:
                qpos = qp * PIECE + lax.broadcasted_iota(jnp.int32, (1, 2 * PIECE), 1) % PIECE
                kpos = kp * PIECE + lax.broadcasted_iota(jnp.int32, (PIECE, 1), 0)
                s = jnp.where((kpos <= qpos) & (kpos >= doc_start(bounds, qpos)), s, NEG_BIG)
            p = jnp.exp2(s).astype(BF16)
            dp = dot(kv_ref[0, :, hd:], do2, NT)
            ds = (p.astype(F32) * (dp - ld_ref[slot, 1:2, :])).astype(BF16)
            dv_ref[...] += dot(p, do2, NN)
            dk_ref[...] += dot(ds, q2, NN)

        masked_or_not(bounds, qp, kp, tile)

    out_ref[0, :, :hd] = dk_ref[...] * scale
    out_ref[0, :, hd:] = dv_ref[...]

    @pl.when(g == pl.num_programs(0) - 1)
    def _():
        for ref, piece, _ in sources:
            qd.need(ref, piece)


def attn_kv(target, sc, ld_all, kvg, qds, n_dev, scale):
    n_piece, _, two_hd = kvg.shape
    hd = two_hd // 2
    last = n_piece - 1
    own = target is None
    n_key = 2 if own else 1

    def kv_block(g, sc):
        me = sc[0]
        if own:
            return (jnp.where(g == 0, me, last - me), 0, 0)
        _, x_chip, y_chip, d_chip, core = chips_of(me)
        return (2 * (x_chip, y_chip, d_chip)[target] + core, 0, 0)

    return pl.pallas_call(
        functools.partial(attn_kv_kernel, n_dev, scale, target),
        grid_spec=pltpu.PrefetchScalarGridSpec(
            num_scalar_prefetch=1,
            grid=(n_key,),
            in_specs=[
                pl.BlockSpec(ld_all.shape, lambda g, sc: (0, 0, 0)),
                pl.BlockSpec((1, PIECE, two_hd), kv_block),
            ] + [ANY] * len(qds),
            out_specs=pl.BlockSpec((1, PIECE, two_hd), lambda g, sc: (g, 0, 0)),
            scratch_shapes=[
                *loader_scratch(n_piece, 4 * hd),
                pltpu.VMEM((PIECE, hd), F32),
                pltpu.VMEM((PIECE, hd), F32),
            ],
        ),
        out_shape=jax.ShapeDtypeStruct((n_key, PIECE, two_hd), F32),
        compiler_params=pltpu.CompilerParams(vmem_limit_bytes=VMEM_LIMIT, dimension_semantics=("arbitrary",)),
        cost_estimate=pl.CostEstimate(flops=(16 if own else 2) * n_piece * PIECE * PIECE * hd, bytes_accessed=kvg.size, transcendentals=0),
        name="attn_kv_own" if own else "attn_kv_back",
    )(sc, ld_all, kvg, *qds)


def dx_kernel(dq_ref, own_ref, rx_ref, ry_ref, rd_ref, w_hbm, dx_ref, lhs, w_s, w_sem):
    qd = dq_ref.shape[1]
    j = pl.program_id(0)

    def block(n):
        rows = pl.ds(pl.multiple_of(n * PIECE, PIECE), PIECE)
        return pltpu.make_async_copy(w_hbm.at[rows], w_s.at[rows], w_sem.at[n])

    @pl.when(j == 0)
    def _():
        for n in range(w_hbm.shape[0] // PIECE):
            block(n).start()
        lhs[:, :qd] = dq_ref[...]
        lhs[:PIECE, qd:] = (own_ref[0] + rx_ref[0] + ry_ref[0] + rd_ref[0]).astype(BF16)
        lhs[PIECE:, qd:] = own_ref[1].astype(BF16)

    block(j).wait()
    dx_ref[...] = dot(lhs[...], w_s[pl.ds(pl.multiple_of(j * PIECE, PIECE), PIECE), :], NT).astype(BF16)


def dx_proj(dq, own, rx, ry, rd, w):
    rows, qd = dq.shape
    d = w.shape[0]
    full = lambda a: pl.BlockSpec(a.shape, lambda j: (0,) * a.ndim)
    return pl.pallas_call(
        dx_kernel,
        grid=(d // PIECE,),
        in_specs=[full(dq), full(own), full(rx), full(ry), full(rd), ANY],
        out_specs=pl.BlockSpec((rows, PIECE), lambda j: (0, j)),
        out_shape=jax.ShapeDtypeStruct((rows, d), BF16),
        scratch_shapes=[pltpu.VMEM((rows, 2 * qd), BF16), pltpu.VMEM(w.shape, BF16), pltpu.SemaphoreType.DMA((d // PIECE,))],
        compiler_params=pltpu.CompilerParams(vmem_limit_bytes=VMEM_LIMIT, dimension_semantics=("arbitrary",)),
        cost_estimate=pl.CostEstimate(flops=4 * rows * d * qd, bytes_accessed=4 * rows * d, transcendentals=0),
        name="dx_proj",
    )(dq, own, rx, ry, rd, w)


def solution(mesh):
    n_dev = mesh.shape['cp']
    row_spec = P(('dp', 'cp'))
    full_spec = P()

    def chip_pairs(pairs):
        return [(2 * a + c, 2 * b + c) for a, b in pairs for c in range(2)]

    up_x, up_y, up_d = (chip_pairs(p) for p in (((0, 1), (2, 3)), ((0, 2), (1, 3)), ((0, 3), (1, 2))))

    def back(pairs):
        return [(b, a) for a, b in pairs]

    def swap(pairs):
        return [(b, b + 1 - 2 * (b % 2)) for _, b in pairs]

    def local_layer(x_in, dy_in, doc_id, w_q, w_k, w_v, w_o):
        d_model = x_in.shape[1]
        hd = w_q.shape[2]
        scale = hd ** -0.5
        wo = w_o.reshape(2 * hd, d_model)
        kvg, own_q, par_q, up_q, w, sc = proj_gather(
            x_in, dy_in, doc_id.reshape(8, -1), w_q, w_k.reshape(d_model, hd), w_v.reshape(d_model, hd), wo, n_dev)
        o, ld, lcol, dcol = attn_fwd(sc, own_q, kvg, n_dev, scale)
        ld_all = ld_gather(ld, n_dev).reshape(-1, ld.shape[1], ld.shape[2])
        up_q, ld_all = lax.optimization_barrier((up_q, ld_all))
        ups = []
        for pairs in (up_d, up_x, up_y):
            ups.append(lax.ppermute(up_q, 'cp', pairs))
        parts, rets = {}, {}
        for n, pairs in ((2, up_d), (1, up_y), (0, up_x)):
            parts[n] = attn_kv(n, sc, ld_all, kvg, (own_q, par_q), n_dev, scale)
            rets[n] = lax.ppermute(parts[n], 'cp', back(pairs))
        dq = attn_dq(sc, own_q, lcol, dcol, kvg, n_dev, scale)
        y_out = dot(o, wo, NN).astype(BF16)
        dq, y_out, *ups = lax.optimization_barrier((dq, y_out, *ups))
        late_q = []
        for a, pairs in zip((ups[1], ups[2], ups[0]), (up_x, up_y, up_d)):
            late_q += [a, lax.ppermute(a, 'cp', swap(pairs))]
        dkv = attn_kv(None, sc, ld_all, kvg, (own_q, par_q, *late_q), n_dev, scale)
        dx = dx_proj(dq, dkv, rets[0], rets[1], rets[2], w)
        return y_out, dx

    return jax.shard_map(local_layer, mesh=mesh,
                         in_specs=(row_spec, row_spec, row_spec, full_spec, full_spec, full_spec, full_spec),
                         out_specs=(row_spec, row_spec), check_vma=False)
```

profile of v0, /device:TPU:3, one launch (start us, length us, event | category | flops | bytes accessed | tf_op | source)
XLA Modules:
  0.0 209.7 jit_solution(3564690868201509194)
XLA Ops:
  0.6 49.3 %proj_gather.1 = (bf16[16,512,512]{2,1,0:T(8,128)(2,1)}, bf16[2,512,1024]{2,1,0:T(8,128)(2,1)}, bf16[2,512,1024]{2,1,0:T(8,128)(2,1)}, bf16[512,1024]{1,0:T(8,12...) custom-call(bf16[1024,3584]{1,0:T(8,128)(2,1)} %x_hbm.1, bf16[1024,3584]{1,0:T(8,128)(2,1)} %dy_hbm.1, s32[8,128]{1,0:T(8,128)} %bitcast.15, ...), custom_call_target="tpu_custom_call" | custom-call | flops 11274289152 | bytes 29360128 | tf_op jit(solution)/shard_map/proj_gather/pallas_call | solution.py:187
  49.9 19.5 %attn_fwd.1 = (bf16[1024,512]{1,0:T(8,128)(2,1)}, f32[2,2,1024]{2,1,0:T(2,128)}, f32[2,1024,128]{2,1,0:T(8,128)}, f32[2,1024,128]{2,1,0:T(8,128)}) custom-call(s32[5]{0:T(128)} %get-tuple-element.19.sc_ref, bf16[2,512,1024]{2,1,0:T(8,128)(2,1)} %get-tuple-element.20.q_ref.refs_0_, bf16[16,512,512]{2,1,0:T(8,128)(2,1)} %get-tuple-element.21.kv_hbm.kv_ref), custom_call_target="tpu_custom_call" | custom-call | flops 8589934592 | bytes 4194304 | tf_op jit(solution)/shard_map/attn_fwd/pallas_call | solution.py:364
  69.4 6.3 %ld_gather.1 = f32[8,2,2,1024]{3,2,1,0:T(2,128)} custom-call(f32[2,2,1024]{2,1,0:T(2,128)} %get-tuple-element.26.ld_ref), custom_call_target="tpu_custom_call" | custom-call | flops 10000000 | bytes 1048576 | tf_op jit(solution)/shard_map/ld_gather/pallas_call | solution.py:221
  75.7 2.3 %collective-permute-start = (bf16[512,1024]{1,0:T(8,128)(2,1)}, bf16[512,1024]{1,0:T(8,128)(2,1)S(1)}, u32[]{:S(2)}, u32[]{:S(2)}) collective-permute-start(bf16[512,1024]{1,0:T(8,128)(2,1)} %get-tuple-element.27), channel_id=1, source_target_pairs={{0,6},{1,7},{2,4},{3,5}} | collective-permute-start | bytes 3145736 | tf_op jit(solution)/shard_map/ppermute | solution.py:643
  78.0 1.3 collective-permute-start.1
  79.3 1.5 collective-permute-start.2
  80.8 9.4 %convolution_convert_fusion = bf16[1024,3584]{1,0:T(8,128)(2,1)} fusion(bf16[1024,512]{1,0:T(8,128)(2,1)} %get-tuple-element.24, bf16[512,3584]{1,0:T(8,128)(2,1)} %bitcast.12), kind=kOutput, calls=%fused_computation | convolution fusion | flops 3761766400 | bytes 12058624 | tf_op jit(solution)/shard_map/dot_general | solution.py:27
  90.2 20.2 %attn_dq.1.dq_ref = bf16[1024,512]{1,0:T(8,128)(2,1)} custom-call(s32[5]{0:T(128)} %get-tuple-element.19.sc_ref, bf16[2,512,1024]{2,1,0:T(8,128)(2,1)} %get-tuple-element.20.q_ref.refs_0_, f32[2,1024,128]{2,1,0:T(8,128)} %get-tuple-element.22.lcol_ref, f32[2,1024,128]{2,1,0:T(8,128)} %get-tuple-element.23.dcol_ref, ...), custom_call_target="tpu_custom_call" | custom-call | flops 12884901888 | bytes 4194304 | tf_op jit(solution)/shard_map/attn_dq/pallas_call | solution.py:436
  110.4 0.0 collective-permute-done.refs_6_
  110.5 14.2 %collective-permute-done.1.refs_2_ = bf16[512,1024]{1,0:T(8,128)(2,1)S(1)} collective-permute-done((bf16[512,1024]{1,0:T(8,128)(2,1)}, bf16[512,1024]{1,0:T(8,128)(2,1)S(1)}, u32[]{:S(2)}, u32[]{:S(2)}) %collective-permute-start.1) | collective-permute-done | bytes 1048608 | tf_op jit(solution)/shard_map/ppermute | solution.py:643
  124.7 3.2 %collective-permute-start.3 = (bf16[512,1024]{1,0:T(8,128)(2,1)S(1)}, bf16[512,1024]{1,0:T(8,128)(2,1)}, u32[]{:S(2)}, u32[]{:S(2)}) collective-permute-start(bf16[512,1024]{1,0:T(8,128)(2,1)S(1)} %collective-permute-done.1.refs_2_), channel_id=1, source_target_pairs={{2,3},{3,2},{6,7},{7,6}} | collective-permute-start | bytes 3145736 | tf_op jit(solution)/shard_map/ppermute | solution.py:653
  127.8 1.7 collective-permute-start.4
  129.5 1.7 collective-permute-start.5
  131.2 7.6 %attn_kv_back.3 = f32[1,512,512]{2,1,0:T(8,128)} custom-call(s32[5]{0:T(128)} %get-tuple-element.19.sc_ref, f32[16,2,1024]{2,1,0:T(2,128)} %bitcast.7, bf16[16,512,512]{2,1,0:T(8,128)(2,1)} %get-tuple-element.21.kv_hbm.kv_ref, bf16[2,512,1024]{2,1,0:T(8,128)(2,1)} %get-tuple-element.20.q_ref.refs_0_, bf16[2,512,1024]{2,1,0:T(8,128)(2,1)} %get-tuple-element.31.refs_1_), custom_call_target="tpu_custom_call" | custom-call | flops 2147483648 | bytes 4194304 | tf_op jit(solution)/shard_map/attn_kv_back/pallas_call | solution.py:555
  138.9 2.3 %collective-permute-start.6 = (f32[1,512,512]{2,1,0:T(8,128)}, f32[1,512,512]{2,1,0:T(8,128)}, u32[]{:S(2)}, u32[]{:S(2)}) collective-permute-start(f32[1,512,512]{2,1,0:T(8,128)} %attn_kv_back.3), channel_id=1, source_target_pairs={{2,0},{3,1},{6,4},{7,5}} | collective-permute-start | bytes 3145736 | tf_op jit(solution)/shard_map/ppermute | solution.py:647
  141.2 3.1 %attn_kv_back.4 = f32[1,512,512]{2,1,0:T(8,128)} custom-call(s32[5]{0:T(128)} %get-tuple-element.19.sc_ref, f32[16,2,1024]{2,1,0:T(2,128)} %bitcast.8, bf16[16,512,512]{2,1,0:T(8,128)(2,1)} %get-tuple-element.21.kv_hbm.kv_ref, bf16[2,512,1024]{2,1,0:T(8,128)(2,1)} %get-tuple-element.20.q_ref.refs_0_, bf16[2,512,1024]{2,1,0:T(8,128)(2,1)} %get-tuple-element.31.refs_1_), custom_call_target="tpu_custom_call" | custom-call | flops 2147483648 | bytes 4194304 | tf_op jit(solution)/shard_map/attn_kv_back/pallas_call | solution.py:555
  144.3 1.5 collective-permute-start.7
  145.8 3.1 %attn_kv_back.5 = f32[1,512,512]{2,1,0:T(8,128)} custom-call(s32[5]{0:T(128)} %get-tuple-element.19.sc_ref, f32[16,2,1024]{2,1,0:T(2,128)} %bitcast.9, bf16[16,512,512]{2,1,0:T(8,128)(2,1)} %get-tuple-element.21.kv_hbm.kv_ref, bf16[2,512,1024]{2,1,0:T(8,128)(2,1)} %get-tuple-element.20.q_ref.refs_0_, bf16[2,512,1024]{2,1,0:T(8,128)(2,1)} %get-tuple-element.31.refs_1_), custom_call_target="tpu_custom_call" | custom-call | flops 2147483648 | bytes 4194304 | tf_op jit(solution)/shard_map/attn_kv_back/pallas_call | solution.py:555
  148.9 1.3 collective-permute-start.8
  150.2 12.2 %attn_kv_own.1.own_ref = f32[2,512,512]{2,1,0:T(8,128)} custom-call(s32[5]{0:T(128)} %get-tuple-element.19.sc_ref, f32[16,2,1024]{2,1,0:T(2,128)} %bitcast.10, bf16[16,512,512]{2,1,0:T(8,128)(2,1)} %get-tuple-element.21.kv_hbm.kv_ref, bf16[2,512,1024]{2,1,0:T(8,128)(2,1)} %get-tuple-element.20.q_ref.refs_0_, ...), custom_call_target="tpu_custom_call" | custom-call | flops 17179869184 | bytes 4194304 | tf_op jit(solution)/shard_map/attn_kv_own/pallas_call | solution.py:555
  162.4 0.9 collective-permute-done.6.rx_ref
  163.3 31.0 %collective-permute-done.7.ry_ref = f32[1,512,512]{2,1,0:T(8,128)} collective-permute-done((f32[1,512,512]{2,1,0:T(8,128)}, f32[1,512,512]{2,1,0:T(8,128)}, u32[]{:S(2)}, u32[]{:S(2)}) %collective-permute-start.7) | collective-permute-done | bytes 1048608 | tf_op jit(solution)/shard_map/ppermute | solution.py:647
  194.3 1.0 copy-done.3
  195.3 14.2 %dx_proj.1 = bf16[1024,3584]{1,0:T(8,128)(2,1)} custom-call(bf16[1024,512]{1,0:T(8,128)(2,1)} %attn_dq.1.dq_ref, f32[2,512,512]{2,1,0:T(8,128)} %attn_kv_own.1.own_ref, f32[1,512,512]{2,1,0:T(8,128)} %collective-permute-done.6.rx_ref, f32[1,512,512]{2,1,0:T(8,128)} %collective-permute-done.7.ry_ref, f32[1,512,512]{2,1,0:T(8,128)} %copy-done.3, ...), custom_call_target="tpu_custom_call" | custom-call | flops 7516192768 | bytes 14680064 | tf_op jit(solution)/shard_map/dx_proj/pallas_call | solution.py:602
  (12 shorter events, 0.0 us)
Async XLA Ops:
  75.7 34.7 %collective-permute-start = (bf16[512,1024]{1,0:T(8,128)(2,1)}, bf16[512,1024]{1,0:T(8,128)(2,1)S(1)}, u32[]{:S(2)}, u32[]{:S(2)}) collective-permute-start(bf16[512,1024]{1,0:T(8,128)(2,1)} %get-tuple-element.27), channel_id=1, source_target_pairs={{0,6},{1,7},{2,4},{3,5}} | collective-permute-start | bytes 3145736 | tf_op jit(solution)/shard_map/ppermute | solution.py:643
  78.0 46.7 %collective-permute-start.1 = (bf16[512,1024]{1,0:T(8,128)(2,1)}, bf16[512,1024]{1,0:T(8,128)(2,1)S(1)}, u32[]{:S(2)}, u32[]{:S(2)}) collective-permute-start(bf16[512,1024]{1,0:T(8,128)(2,1)} %get-tuple-element.27), channel_id=1, source_target_pairs={{0,2},{1,3},{4,6},{5,7}} | collective-permute-start | bytes 3145736 | tf_op jit(solution)/shard_map/ppermute | solution.py:643
  79.3 45.4 %collective-permute-start.2 = (bf16[512,1024]{1,0:T(8,128)(2,1)}, bf16[512,1024]{1,0:T(8,128)(2,1)S(1)}, u32[]{:S(2)}, u32[]{:S(2)}) collective-permute-start(bf16[512,1024]{1,0:T(8,128)(2,1)} %get-tuple-element.27), channel_id=1, source_target_pairs={{0,4},{1,5},{2,6},{3,7}} | collective-permute-start | bytes 3145736 | tf_op jit(solution)/shard_map/ppermute | solution.py:643
  110.5 28.4 %copy-start = (bf16[512,1024]{1,0:T(8,128)(2,1)}, bf16[512,1024]{1,0:T(8,128)(2,1)S(1)}, u32[]{:S(2)}) copy-start(bf16[512,1024]{1,0:T(8,128)(2,1)S(1)} %collective-permute-done.refs_6_) | copy-start | bytes 3145732
  124.7 14.2 %copy-start.1 = (bf16[512,1024]{1,0:T(8,128)(2,1)}, bf16[512,1024]{1,0:T(8,128)(2,1)S(1)}, u32[]{:S(2)}) copy-start(bf16[512,1024]{1,0:T(8,128)(2,1)S(1)} %collective-permute-done.1.refs_2_) | copy-start | bytes 3145732
  124.7 14.2 %copy-start.2 = (bf16[512,1024]{1,0:T(8,128)(2,1)}, bf16[512,1024]{1,0:T(8,128)(2,1)S(1)}, u32[]{:S(2)}) copy-start(bf16[512,1024]{1,0:T(8,128)(2,1)S(1)} %collective-permute-done.2.refs_4_) | copy-start | bytes 3145732
  124.7 24.2 %collective-permute-start.3 = (bf16[512,1024]{1,0:T(8,128)(2,1)S(1)}, bf16[512,1024]{1,0:T(8,128)(2,1)}, u32[]{:S(2)}, u32[]{:S(2)}) collective-permute-start(bf16[512,1024]{1,0:T(8,128)(2,1)S(1)} %collective-permute-done.1.refs_2_), channel_id=1, source_target_pairs={{2,3},{3,2},{6,7},{7,6}} | collective-permute-start | bytes 3145736 | tf_op jit(solution)/shard_map/ppermute | solution.py:653
  127.8 22.4 %collective-permute-start.4 = (bf16[512,1024]{1,0:T(8,128)(2,1)S(1)}, bf16[512,1024]{1,0:T(8,128)(2,1)}, u32[]{:S(2)}, u32[]{:S(2)}) collective-permute-start(bf16[512,1024]{1,0:T(8,128)(2,1)S(1)} %collective-permute-done.2.refs_4_), channel_id=1, source_target_pairs={{4,5},{5,4},{6,7},{7,6}} | collective-permute-start | bytes 3145736 | tf_op jit(solution)/shard_map/ppermute | solution.py:653
  129.5 20.7 %collective-permute-start.5 = (bf16[512,1024]{1,0:T(8,128)(2,1)S(1)}, bf16[512,1024]{1,0:T(8,128)(2,1)}, u32[]{:S(2)}, u32[]{:S(2)}) collective-permute-start(bf16[512,1024]{1,0:T(8,128)(2,1)S(1)} %collective-permute-done.refs_6_), channel_id=1, source_target_pairs={{6,7},{7,6},{4,5},{5,4}} | collective-permute-start | bytes 3145736 | tf_op jit(solution)/shard_map/ppermute | solution.py:653
  138.9 24.4 %collective-permute-start.6 = (f32[1,512,512]{2,1,0:T(8,128)}, f32[1,512,512]{2,1,0:T(8,128)}, u32[]{:S(2)}, u32[]{:S(2)}) collective-permute-start(f32[1,512,512]{2,1,0:T(8,128)} %attn_kv_back.3), channel_id=1, source_target_pairs={{2,0},{3,1},{6,4},{7,5}} | collective-permute-start | bytes 3145736 | tf_op jit(solution)/shard_map/ppermute | solution.py:647
  144.3 50.0 %collective-permute-start.7 = (f32[1,512,512]{2,1,0:T(8,128)}, f32[1,512,512]{2,1,0:T(8,128)}, u32[]{:S(2)}, u32[]{:S(2)}) collective-permute-start(f32[1,512,512]{2,1,0:T(8,128)} %attn_kv_back.4), channel_id=1, source_target_pairs={{4,0},{5,1},{6,2},{7,3}} | collective-permute-start | bytes 3145736 | tf_op jit(solution)/shard_map/ppermute | solution.py:647
  148.9 45.4 %collective-permute-start.8 = (f32[1,512,512]{2,1,0:T(8,128)}, f32[1,512,512]{2,1,0:T(8,128)S(1)}, u32[]{:S(2)}, u32[]{:S(2)}) collective-permute-start(f32[1,512,512]{2,1,0:T(8,128)} %attn_kv_back.5), channel_id=1, source_target_pairs={{6,0},{7,1},{4,2},{5,3}} | collective-permute-start | bytes 3145736 | tf_op jit(solution)/shard_map/ppermute | solution.py:647
  194.3 1.0 copy-start.3
where the time goes:
time: 210 us
  Pallas kernels  136 us (65%)
  waiting for transfers between devices  46.1 us (22%)
  starting transfers between devices  16.7 us (8%)
  matrix products  9.37 us (4%)
    pallas_call x1, Pallas kernels, proj_gather(): pl.pallas_call(functools.partial(proj_gather_kernel, n_dev), in_specs=[AN...  49.3 us
    ppermute x3, waiting for transfers between devices, local_layer(): rets[n] = lax.ppermute(parts[n], 'cp', back(pairs))  31.9 us
    pallas_call x4, Pallas kernels, attn_kv(): pl.pallas_call(functools.partial(attn_kv_kernel, n_dev, scale, target), g...  26 us
    pallas_call x1, Pallas kernels, attn_dq(): pl.pallas_call(functools.partial(attn_dq_kernel, n_dev, scale), grid_spec...  20.2 us
    pallas_call x1, Pallas kernels, attn_fwd(): pl.pallas_call(functools.partial(attn_fwd_kernel, n_dev, scale), grid_spe...  19.5 us
    pallas_call x1, Pallas kernels, dx_proj(): pl.pallas_call(dx_kernel, grid=(d // PIECE,), in_specs=[full(dq), full(ow...  14.2 us
    ppermute x3, waiting for transfers between devices, local_layer(): ups.append(lax.ppermute(up_q, 'cp', pairs))  14.2 us
    dot_general x1, matrix products, dot(): return lax.dot_general(a, b, dims, preferred_element_type=F32)  9.37 us
  transfers between devices with their start and end apart: 9, of which 3 were waited for; matrix products, arithmetic and copies ran while one was open for 4% of the time, Pallas kernels for 22%

commit v1 on v0

--- a/solution.py
+++ b/solution.py
@@ -17,7 +17,8 @@
 LANES = 128
 NT = (((1,), (1,)), ((), ()))
 NN = (((1,), (0,)), ((), ()))
-VMEM_LIMIT = 60 * 1024 * 1024
+MIB = 1 << 20
+VMEM_LIMIT = 60 * MIB
 MESH = pl.DeviceIdType.MESH
 ANY = pl.BlockSpec(memory_space=pl.ANY)
 VMEM = pl.BlockSpec(memory_space=pltpu.VMEM)
@@ -646,11 +647,11 @@
             parts[n] = attn_kv(n, sc, ld_all, kvg, (own_q, par_q), n_dev, scale)
             rets[n] = lax.ppermute(parts[n], 'cp', back(pairs))
         dq = attn_dq(sc, own_q, lcol, dcol, kvg, n_dev, scale)
+        dq, *ups = lax.optimization_barrier((dq, *ups))
+        late_q = []
+        for a, pairs in ((ups[1], up_x), (ups[2], up_y), (ups[0], up_d)):
+            late_q += [a, lax.ppermute(a, 'cp', swap(pairs))]
         y_out = dot(o, wo, NN).astype(BF16)
-        dq, y_out, *ups = lax.optimization_barrier((dq, y_out, *ups))
-        late_q = []
-        for a, pairs in zip((ups[1], ups[2], ups[0]), (up_x, up_y, up_d)):
-            late_q += [a, lax.ppermute(a, 'cp', swap(pairs))]
         dkv = attn_kv(None, sc, ld_all, kvg, (own_q, par_q, *late_q), n_dev, scale)
         dx = dx_proj(dq, dkv, rets[0], rets[1], rets[2], w)
         return y_out, dx

time: 210 us -> 201 us (0.957)
  the two profiles are of different devices: /device:TPU:3 before, /device:TPU:0 now
where the time goes in v1:
time: 201 us; the launch traced here: 200 us
  Pallas kernels  130 us (65%)
  waiting for transfers between devices  41.3 us (21%)
  starting transfers between devices  18 us (9%)
  matrix products  9.45 us (5%)
    pallas_call x1, Pallas kernels, proj_gather(): pl.pallas_call(functools.partial(proj_gather_kernel, n_dev), in_specs=[AN...  50.5 us
    ppermute x3, waiting for transfers between devices, local_layer(): rets[n] = lax.ppermute(parts[n], 'cp', back(pairs))  23.7 us
    pallas_call x1, Pallas kernels, attn_dq(): pl.pallas_call(functools.partial(attn_dq_kernel, n_dev, scale), grid_spec...  19.6 us
    pallas_call x4, Pallas kernels, attn_kv(): pl.pallas_call(functools.partial(attn_kv_kernel, n_dev, scale, target), g...  19.2 us
    pallas_call x1, Pallas kernels, attn_fwd(): pl.pallas_call(functools.partial(attn_fwd_kernel, n_dev, scale), grid_spe...  18.6 us
    ppermute x3, waiting for transfers between devices, local_layer(): ups.append(lax.ppermute(up_q, 'cp', pairs))  17.6 us
    pallas_call x1, Pallas kernels, dx_proj(): pl.pallas_call(dx_kernel, grid=(d // PIECE,), in_specs=[full(dq), full(ow...  14.3 us
    dot_general x1, matrix products, dot(): return lax.dot_general(a, b, dims, preferred_element_type=F32)  9.45 us
  transfers between devices with their start and end apart: 9, of which 3 were waited for; matrix products, arithmetic and copies ran while one was open for 5% of the time, Pallas kernels for 19%

profile of v1, /device:TPU:0, one launch (start us, length us, event | category | flops | bytes accessed | tf_op | source)
XLA Modules:
  0.0 199.5 jit_solution(12268128221830196015)
XLA Ops:
  0.6 50.5 %proj_gather.1 = (bf16[16,512,512]{2,1,0:T(8,128)(2,1)}, bf16[2,512,1024]{2,1,0:T(8,128)(2,1)}, bf16[2,512,1024]{2,1,0:T(8,128)(2,1)}, bf16[512,1024]{1,0:T(8,12...) custom-call(bf16[1024,3584]{1,0:T(8,128)(2,1)} %x_hbm.1, bf16[1024,3584]{1,0:T(8,128)(2,1)} %dy_hbm.1, s32[8,128]{1,0:T(8,128)} %bitcast.15, ...), custom_call_target="tpu_custom_call" | custom-call | flops 11274289152 | bytes 29360128 | tf_op jit(solution)/shard_map/proj_gather/pallas_call | solution.py:188
  51.2 18.6 %attn_fwd.1 = (bf16[1024,512]{1,0:T(8,128)(2,1)}, f32[2,2,1024]{2,1,0:T(2,128)}, f32[2,1024,128]{2,1,0:T(8,128)}, f32[2,1024,128]{2,1,0:T(8,128)}) custom-call(s32[5]{0:T(128)} %get-tuple-element.18.sc_ref, bf16[2,512,1024]{2,1,0:T(8,128)(2,1)} %get-tuple-element.19.q_ref.refs_0_, bf16[16,512,512]{2,1,0:T(8,128)(2,1)} %get-tuple-element.20.kv_hbm.kv_ref), custom_call_target="tpu_custom_call" | custom-call | flops 8589934592 | bytes 4194304 | tf_op jit(solution)/shard_map/attn_fwd/pallas_call | solution.py:365
  69.8 7.5 %ld_gather.1 = f32[8,2,2,1024]{3,2,1,0:T(2,128)} custom-call(f32[2,2,1024]{2,1,0:T(2,128)} %get-tuple-element.25.ld_ref), custom_call_target="tpu_custom_call" | custom-call | flops 10000000 | bytes 1048576 | tf_op jit(solution)/shard_map/ld_gather/pallas_call | solution.py:222
  77.3 2.5 %collective-permute-start.2 = (bf16[512,1024]{1,0:T(8,128)(2,1)}, bf16[512,1024]{1,0:T(8,128)(2,1)S(1)}, u32[]{:S(2)}, u32[]{:S(2)}) collective-permute-start(bf16[512,1024]{1,0:T(8,128)(2,1)} %get-tuple-element.26), channel_id=1, source_target_pairs={{0,4},{1,5},{2,6},{3,7}} | collective-permute-start | bytes 3145736 | tf_op jit(solution)/shard_map/ppermute | solution.py:644
  79.8 4.4 %collective-permute-start.1 = (bf16[512,1024]{1,0:T(8,128)(2,1)}, bf16[512,1024]{1,0:T(8,128)(2,1)}, u32[]{:S(2)}, u32[]{:S(2)}) collective-permute-start(bf16[512,1024]{1,0:T(8,128)(2,1)} %get-tuple-element.26), channel_id=1, source_target_pairs={{0,2},{1,3},{4,6},{5,7}} | collective-permute-start | bytes 3145736 | tf_op jit(solution)/shard_map/ppermute | solution.py:644
  84.2 2.4 %collective-permute-start = (bf16[512,1024]{1,0:T(8,128)(2,1)}, bf16[512,1024]{1,0:T(8,128)(2,1)}, u32[]{:S(2)}, u32[]{:S(2)}) collective-permute-start(bf16[512,1024]{1,0:T(8,128)(2,1)} %get-tuple-element.26), channel_id=1, source_target_pairs={{0,6},{1,7},{2,4},{3,5}} | collective-permute-start | bytes 3145736 | tf_op jit(solution)/shard_map/ppermute | solution.py:644
  86.6 3.3 %attn_kv_back.3 = f32[1,512,512]{2,1,0:T(8,128)} custom-call(s32[5]{0:T(128)} %get-tuple-element.18.sc_ref, f32[16,2,1024]{2,1,0:T(2,128)} %bitcast.7, bf16[16,512,512]{2,1,0:T(8,128)(2,1)} %get-tuple-element.20.kv_hbm.kv_ref, bf16[2,512,1024]{2,1,0:T(8,128)(2,1)} %get-tuple-element.19.q_ref.refs_0_, bf16[2,512,1024]{2,1,0:T(8,128)(2,1)} %get-tuple-element.29.refs_1_), custom_call_target="tpu_custom_call" | custom-call | flops 2147483648 | bytes 4194304 | tf_op jit(solution)/shard_map/attn_kv_back/pallas_call | solution.py:556
  89.8 1.3 collective-permute-start.6
  91.1 19.6 %attn_dq.1.dq_ref = bf16[1024,512]{1,0:T(8,128)(2,1)} custom-call(s32[5]{0:T(128)} %get-tuple-element.18.sc_ref, bf16[2,512,1024]{2,1,0:T(8,128)(2,1)} %get-tuple-element.19.q_ref.refs_0_, f32[2,1024,128]{2,1,0:T(8,128)} %get-tuple-element.22.lcol_ref, f32[2,1024,128]{2,1,0:T(8,128)} %get-tuple-element.23.dcol_ref, ...), custom_call_target="tpu_custom_call" | custom-call | flops 12884901888 | bytes 4194304 | tf_op jit(solution)/shard_map/attn_dq/pallas_call | solution.py:437
  110.7 14.5 %collective-permute-done.2.refs_4_ = bf16[512,1024]{1,0:T(8,128)(2,1)S(1)} collective-permute-done((bf16[512,1024]{1,0:T(8,128)(2,1)}, bf16[512,1024]{1,0:T(8,128)(2,1)S(1)}, u32[]{:S(2)}, u32[]{:S(2)}) %collective-permute-start.2) | collective-permute-done | bytes 1048608 | tf_op jit(solution)/shard_map/ppermute | solution.py:644
  125.2 0.0 collective-permute-done.1.refs_2_
  125.2 3.2 %collective-permute-done.refs_6_ = bf16[512,1024]{1,0:T(8,128)(2,1)} collective-permute-done((bf16[512,1024]{1,0:T(8,128)(2,1)}, bf16[512,1024]{1,0:T(8,128)(2,1)}, u32[]{:S(2)}, u32[]{:S(2)}) %collective-permute-start) | collective-permute-done | bytes 1048608 | tf_op jit(solution)/shard_map/ppermute | solution.py:644
  128.4 1.6 collective-permute-start.3
  130.0 1.6 collective-permute-start.4
  131.7 1.6 collective-permute-start.5
  133.3 3.1 %attn_kv_back.4 = f32[1,512,512]{2,1,0:T(8,128)} custom-call(s32[5]{0:T(128)} %get-tuple-element.18.sc_ref, f32[16,2,1024]{2,1,0:T(2,128)} %bitcast.8, bf16[16,512,512]{2,1,0:T(8,128)(2,1)} %get-tuple-element.20.kv_hbm.kv_ref, bf16[2,512,1024]{2,1,0:T(8,128)(2,1)} %get-tuple-element.19.q_ref.refs_0_, bf16[2,512,1024]{2,1,0:T(8,128)(2,1)} %get-tuple-element.29.refs_1_), custom_call_target="tpu_custom_call" | custom-call | flops 2147483648 | bytes 4194304 | tf_op jit(solution)/shard_map/attn_kv_back/pallas_call | solution.py:556
  136.4 1.3 collective-permute-start.7
  137.7 3.3 %attn_kv_back.5 = f32[1,512,512]{2,1,0:T(8,128)} custom-call(s32[5]{0:T(128)} %get-tuple-element.18.sc_ref, f32[16,2,1024]{2,1,0:T(2,128)} %bitcast.9, bf16[16,512,512]{2,1,0:T(8,128)(2,1)} %get-tuple-element.20.kv_hbm.kv_ref, bf16[2,512,1024]{2,1,0:T(8,128)(2,1)} %get-tuple-element.19.q_ref.refs_0_, bf16[2,512,1024]{2,1,0:T(8,128)(2,1)} %get-tuple-element.29.refs_1_), custom_call_target="tpu_custom_call" | custom-call | flops 2147483648 | bytes 4194304 | tf_op jit(solution)/shard_map/attn_kv_back/pallas_call | solution.py:556
  141.0 9.5 %convolution_convert_fusion = bf16[1024,3584]{1,0:T(8,128)(2,1)} fusion(bf16[1024,512]{1,0:T(8,128)(2,1)} %get-tuple-element.21, bf16[512,3584]{1,0:T(8,128)(2,1)} %bitcast.12), kind=kOutput, calls=%fused_computation | convolution fusion | flops 3761766400 | bytes 12058624 | tf_op jit(solution)/shard_map/dot_general | solution.py:28
  150.5 0.0 collective-permute-done.3.refs_3_
  150.5 1.3 collective-permute-start.8
  151.8 9.6 %attn_kv_own.1.own_ref = f32[2,512,512]{2,1,0:T(8,128)} custom-call(s32[5]{0:T(128)} %get-tuple-element.18.sc_ref, f32[16,2,1024]{2,1,0:T(2,128)} %bitcast.10, bf16[16,512,512]{2,1,0:T(8,128)(2,1)} %get-tuple-element.20.kv_hbm.kv_ref, bf16[2,512,1024]{2,1,0:T(8,128)(2,1)} %get-tuple-element.19.q_ref.refs_0_, ...), custom_call_target="tpu_custom_call" | custom-call | flops 17179869184 | bytes 4194304 | tf_op jit(solution)/shard_map/attn_kv_own/pallas_call | solution.py:556
  161.4 23.7 %collective-permute-done.7.ry_ref = f32[1,512,512]{2,1,0:T(8,128)} collective-permute-done((f32[1,512,512]{2,1,0:T(8,128)}, f32[1,512,512]{2,1,0:T(8,128)}, u32[]{:S(2)}, u32[]{:S(2)}) %collective-permute-start.7) | collective-permute-done | bytes 1048608 | tf_op jit(solution)/shard_map/ppermute | solution.py:648
  185.1 14.3 %dx_proj.1 = bf16[1024,3584]{1,0:T(8,128)(2,1)} custom-call(bf16[1024,512]{1,0:T(8,128)(2,1)} %attn_dq.1.dq_ref, f32[2,512,512]{2,1,0:T(8,128)} %attn_kv_own.1.own_ref, f32[1,512,512]{2,1,0:T(8,128)} %copy-done.1, f32[1,512,512]{2,1,0:T(8,128)} %collective-permute-done.7.ry_ref, f32[1,512,512]{2,1,0:T(8,128)} %collective-permute-done.8.rd_ref, ...), custom_call_target="tpu_custom_call" | custom-call | flops 7516192768 | bytes 14680064 | tf_op jit(solution)/shard_map/dx_proj/pallas_call | solution.py:603
  (10 shorter events, 0.0 us)
Async XLA Ops:
  77.3 47.9 %collective-permute-start.2 = (bf16[512,1024]{1,0:T(8,128)(2,1)}, bf16[512,1024]{1,0:T(8,128)(2,1)S(1)}, u32[]{:S(2)}, u32[]{:S(2)}) collective-permute-start(bf16[512,1024]{1,0:T(8,128)(2,1)} %get-tuple-element.26), channel_id=1, source_target_pairs={{0,4},{1,5},{2,6},{3,7}} | collective-permute-start | bytes 3145736 | tf_op jit(solution)/shard_map/ppermute | solution.py:644
  79.8 45.4 %collective-permute-start.1 = (bf16[512,1024]{1,0:T(8,128)(2,1)}, bf16[512,1024]{1,0:T(8,128)(2,1)}, u32[]{:S(2)}, u32[]{:S(2)}) collective-permute-start(bf16[512,1024]{1,0:T(8,128)(2,1)} %get-tuple-element.26), channel_id=1, source_target_pairs={{0,2},{1,3},{4,6},{5,7}} | collective-permute-start | bytes 3145736 | tf_op jit(solution)/shard_map/ppermute | solution.py:644
  84.2 44.2 %collective-permute-start = (bf16[512,1024]{1,0:T(8,128)(2,1)}, bf16[512,1024]{1,0:T(8,128)(2,1)}, u32[]{:S(2)}, u32[]{:S(2)}) collective-permute-start(bf16[512,1024]{1,0:T(8,128)(2,1)} %get-tuple-element.26), channel_id=1, source_target_pairs={{0,6},{1,7},{2,4},{3,5}} | collective-permute-start | bytes 3145736 | tf_op jit(solution)/shard_map/ppermute | solution.py:644
  89.8 71.6 %collective-permute-start.6 = (f32[1,512,512]{2,1,0:T(8,128)}, f32[1,512,512]{2,1,0:T(8,128)S(1)}, u32[]{:S(2)}, u32[]{:S(2)}) collective-permute-start(f32[1,512,512]{2,1,0:T(8,128)} %attn_kv_back.3), channel_id=1, source_target_pairs={{2,0},{3,1},{6,4},{7,5}} | collective-permute-start | bytes 3145736 | tf_op jit(solution)/shard_map/ppermute | solution.py:648
  125.2 11.1 %copy-start.2 = (bf16[512,1024]{1,0:T(8,128)(2,1)}, bf16[512,1024]{1,0:T(8,128)(2,1)S(1)}, u32[]{:S(2)}) copy-start(bf16[512,1024]{1,0:T(8,128)(2,1)S(1)} %collective-permute-done.2.refs_4_) | copy-start | bytes 3145732
  128.4 22.1 %collective-permute-start.3 = (bf16[512,1024]{1,0:T(8,128)(2,1)}, bf16[512,1024]{1,0:T(8,128)(2,1)}, u32[]{:S(2)}, u32[]{:S(2)}) collective-permute-start(bf16[512,1024]{1,0:T(8,128)(2,1)} %collective-permute-done.1.refs_2_), channel_id=1, source_target_pairs={{2,3},{3,2},{6,7},{7,6}} | collective-permute-start | bytes 3145736 | tf_op jit(solution)/shard_map/ppermute | solution.py:653
  130.0 21.7 %collective-permute-start.4 = (bf16[512,1024]{1,0:T(8,128)(2,1)S(1)}, bf16[512,1024]{1,0:T(8,128)(2,1)}, u32[]{:S(2)}, u32[]{:S(2)}) collective-permute-start(bf16[512,1024]{1,0:T(8,128)(2,1)S(1)} %collective-permute-done.2.refs_4_), channel_id=1, source_target_pairs={{4,5},{5,4},{6,7},{7,6}} | collective-permute-start | bytes 3145736 | tf_op jit(solution)/shard_map/ppermute | solution.py:653
  131.7 20.1 %collective-permute-start.5 = (bf16[512,1024]{1,0:T(8,128)(2,1)}, bf16[512,1024]{1,0:T(8,128)(2,1)}, u32[]{:S(2)}, u32[]{:S(2)}) collective-permute-start(bf16[512,1024]{1,0:T(8,128)(2,1)} %collective-permute-done.refs_6_), channel_id=1, source_target_pairs={{6,7},{7,6},{4,5},{5,4}} | collective-permute-start | bytes 3145736 | tf_op jit(solution)/shard_map/ppermute | solution.py:653
  136.4 48.7 %collective-permute-start.7 = (f32[1,512,512]{2,1,0:T(8,128)}, f32[1,512,512]{2,1,0:T(8,128)}, u32[]{:S(2)}, u32[]{:S(2)}) collective-permute-start(f32[1,512,512]{2,1,0:T(8,128)} %attn_kv_back.4), channel_id=1, source_target_pairs={{4,0},{5,1},{6,2},{7,3}} | collective-permute-start | bytes 3145736 | tf_op jit(solution)/shard_map/ppermute | solution.py:648
  141.0 9.5 %copy-start = (f32[1,512,512]{2,1,0:T(8,128)S(1)}, f32[1,512,512]{2,1,0:T(8,128)}, u32[]{:S(2)}) copy-start(f32[1,512,512]{2,1,0:T(8,128)} %attn_kv_back.5) | copy-start | bytes 3145732
  150.5 34.6 %collective-permute-start.8 = (f32[1,512,512]{2,1,0:T(8,128)S(1)}, f32[1,512,512]{2,1,0:T(8,128)}, u32[]{:S(2)}, u32[]{:S(2)}) collective-permute-start(f32[1,512,512]{2,1,0:T(8,128)S(1)} %copy-done), channel_id=1, source_target_pairs={{6,0},{7,1},{4,2},{5,3}} | collective-permute-start | bytes 3145736 | tf_op jit(solution)/shard_map/ppermute | solution.py:648
  161.4 23.7 %copy-start.1 = (f32[1,512,512]{2,1,0:T(8,128)}, f32[1,512,512]{2,1,0:T(8,128)S(1)}, u32[]{:S(2)}) copy-start(f32[1,512,512]{2,1,0:T(8,128)S(1)} %collective-permute-done.6.rx_ref) | copy-start | bytes 3145732
